TPU v7x, 32 devices: a whole 2x2x4 slice. The times are simulated.
32 devices in a mesh: rep: 2 (over x), tp: 4 (over z), pp: 4 (over y, core).
Axes of the slice: x: 2, y: 2, z: 4, core: 2. Of those that a mesh axis runs over, the one named last changes fastest.
Arguments:
- w_gate: bfloat16 [4, 896, 4864], P('pp', None, 'tp')
- w_up: bfloat16 [4, 896, 4864], P('pp', None, 'tp')
- w_down: bfloat16 [4, 4864, 896], P('pp', 'tp')
- norm_gain: bfloat16 [4, 896], P('pp')
- a_up: bfloat16 [4, 12, 896, 32], P('pp', 'rep'), parts along dimension 1
- b_up: bfloat16 [4, 12, 32, 4864], P('pp', 'rep', None, 'tp'), parts along dimension 1
- a_down: bfloat16 [4, 12, 4864, 32], P('pp', 'rep', 'tp'), parts along dimension 1
- b_down: bfloat16 [4, 12, 32, 896], P('pp', 'rep'), parts along dimension 1
- inputs: bfloat16 [12, 3, 2, 64, 896], P('rep'), parts along dimension 0
- targets: bfloat16 [12, 3, 2, 64, 896], P('rep'), parts along dimension 0
- lengths: int32 [12, 3, 2], P('rep'), parts along dimension 0
Outputs:
- output 1: float32 [12], P('rep'), parts along dimension 0
- output 2: float32 [4, 12, 896, 32], P('pp', 'rep'), parts along dimension 1
- output 3: float32 [4, 12, 32, 4864], P('pp', 'rep', None, 'tp'), parts along dimension 1
- output 4: float32 [4, 12, 4864, 32], P('pp', 'rep', 'tp'), parts along dimension 1
- output 5: float32 [4, 12, 32, 896], P('pp', 'rep'), parts along dimension 1
There are 2 independent parts. A program takes and returns all parts, laid end to end along the dimension named above; an argument that names none is the same for every part.
All inputs are finite; a program needn't handle non-finite values.
Results may differ from a plain program's by a relative error of at most 0.0197842.
Values are sent between devices in bfloat16 or wider.
A program may use at most 1 GiB of HBM per device.

v0:
```python
import functools

import jax
import jax.numpy as jnp
import numpy as np
from jax import lax
from jax.experimental import pallas as pl
from jax.experimental.pallas import tpu as pltpu
from jax.sharding import PartitionSpec as P

LORA_SCALE = 2.0
NORM_EPS = 1e-5
UNIT = 128
LANES = 256
FOLD = 128
PLANS = ((10,), (12,), (9, 9))
MESH_ID = pl.DeviceIdType.MESH
F32 = jnp.float32
BF16 = jnp.bfloat16


def dot_nn(lhs, rhs):
    return lax.dot_general(lhs, rhs, (((1,), (0,)), ((), ())), preferred_element_type=F32)


def dot_nt(lhs, rhs):
    return lax.dot_general(lhs, rhs, (((1,), (1,)), ((), ())), preferred_element_type=F32)


def dot_tn(lhs, rhs):
    return lax.dot_general(lhs, rhs, (((0,), (0,)), ((), ())), preferred_element_type=F32)


def fold(wide):
    return wide[:, :FOLD] + wide[:, FOLD:]


def unfold(folded, mask):
    return jnp.concatenate([folded, folded], axis=1) * mask


def sweep_kernel(units, stages,
                 w_gate, w_up, w_down, gain, a_up_hbm, b_up_hbm, a_down_hbm, b_down_hbm, rows_hbm, mask, weight,
                 loss_out, g_a_up, g_b_up, g_a_down, g_b_down,
                 h_in, g_in, gate_s, up_s, low_s, c_s, l_s, p_in, pl_in, s_in, sl_in, part, p_out, pl_out, s_out, sl_out, h_out, q_s, gup_s, gld_s, loss_in,
                 a_up, b_up, a_down, b_down, load_sem, adapter_sem, p_sem, pl_sem, s_sem, sl_sem, h_sem, g_sem, c_sem, l_sem, loss_sem,
                 p_send, pl_send, s_send, sl_send, h_send, c_send, l_send, g_send, loss_send):
    d_model = h_in.shape[2]
    used = g_a_up.shape[0]
    tp_idx = lax.axis_index("tp")
    stage = lax.axis_index("pp")
    last = stages - 1
    is_mid = lax.div(tp_idx + 1, 2) == 1
    is_end = lax.div(tp_idx + 1, 2) != 1
    mid_idx = 1 + lax.div(tp_idx, 2)
    end_idx = 3 * lax.div(tp_idx, 2)
    later = lax.rem(stage + 1, stages)
    earlier = lax.rem(stage + stages - 1, stages)
    cross_idx = 3 - tp_idx
    is_first = stage == 0
    is_last = stage == last

    def remote(src, dst, send, recv, tp_to, pp_to):
        return pltpu.make_async_remote_copy(src_ref=src, dst_ref=dst, send_sem=send, recv_sem=recv,
                                            device_id={"tp": tp_to, "pp": pp_to}, device_id_type=MESH_ID)

    load_inputs = pltpu.make_async_copy(rows_hbm, h_in, load_sem)
    load_targets = pltpu.make_async_copy(rows_hbm, g_in, load_sem)

    @pl.when(is_first)
    def _():
        load_inputs.start()

    @pl.when(is_last & is_mid)
    def _():
        load_targets.start()

    adapters = [(a_up_hbm, a_up), (b_up_hbm, b_up), (a_down_hbm, a_down), (b_down_hbm, b_down)]
    adapter_loads = [pltpu.make_async_copy(src, dst.at[pl.ds(0, used)], adapter_sem.at[which])
                     for which, (src, dst) in enumerate(adapters)]
    for load in adapter_loads:
        load.start()
    for _, dst in adapters:
        dst[pl.ds(used, LANES - used), :] = jnp.zeros((LANES - used, dst.shape[1]), BF16)

    barrier = pltpu.get_barrier_semaphore()

    def greet(tp_to, pp_to):
        pl.semaphore_signal(barrier, inc=1, device_id={"tp": tp_to, "pp": pp_to}, device_id_type=MESH_ID)

    @pl.when(is_mid)
    def _():
        greet(end_idx, stage)
        greet(cross_idx, stage)

        @pl.when(stage < last)
        def _():
            greet(mid_idx, later)
            greet(end_idx, later)

        @pl.when(stage > 0)
        def _():
            greet(mid_idx, earlier)
            greet(end_idx, earlier)

        pl.semaphore_wait(barrier, 2 + 2 * (stage < last).astype(jnp.int32) + 2 * (stage > 0).astype(jnp.int32))

    @pl.when(is_end)
    def _():
        greet(mid_idx, stage)

        @pl.when(stage < last)
        def _():
            greet(mid_idx, later)

        @pl.when(stage > 0)
        def _():
            greet(mid_idx, earlier)

        pl.semaphore_wait(barrier, 1 + (stage < last).astype(jnp.int32) + (stage > 0).astype(jnp.int32))

    loss_out[...] = jnp.zeros_like(loss_out)
    g_a_up[...] = jnp.zeros_like(g_a_up)
    g_b_up[...] = jnp.zeros_like(g_b_up)
    g_a_down[...] = jnp.zeros_like(g_a_down)
    g_b_down[...] = jnp.zeros_like(g_b_down)

    for load in adapter_loads:
        load.wait()

    @pl.when(is_first)
    def _():
        load_inputs.wait()

    @pl.when(is_last & is_mid)
    def _():
        load_targets.wait()

    def part_copy(idx, slot):
        return remote(p_out.at[slot], p_in.at[idx], p_send.at[slot], p_sem.at[idx], mid_idx, stage)

    def part_low_copy(idx, slot):
        return remote(pl_out.at[slot], pl_in.at[idx], pl_send.at[slot], pl_sem.at[idx], mid_idx, stage)

    def sum_copy(idx, slot):
        land = 2 * idx + lax.div(slot, 2)
        return remote(s_out.at[slot], s_in.at[land], s_send.at[slot], s_sem.at[land], cross_idx, stage)

    def sum_low_copy(idx, slot):
        land = 2 * idx + lax.div(slot, 2)
        return remote(sl_out.at[slot], sl_in.at[land], sl_send.at[slot], sl_sem.at[land], cross_idx, stage)

    def hidden_copy(idx, slot, which):
        return remote(h_out.at[slot], h_in.at[idx], h_send.at[slot, which], h_sem.at[idx],
                      (mid_idx, end_idx)[which], later)

    def grad_copy(idx, slot, which):
        return remote(h_out.at[slot], g_in.at[idx], h_send.at[slot, which], g_sem.at[idx],
                      (mid_idx, end_idx)[which], earlier)

    def top_copy(idx):
        return remote(g_in.at[idx], g_in.at[idx], g_send.at[idx], g_sem.at[idx], end_idx, stage)

    def c_copy(idx):
        return remote(c_s.at[idx], c_s.at[idx], c_send.at[idx], c_sem.at[idx], end_idx, stage)

    def l_copy(idx):
        return remote(l_s.at[idx], l_s.at[idx], l_send.at[idx], l_sem.at[idx], end_idx, stage)

    def loss_copy(which):
        return remote(loss_out, loss_in, loss_send.at[which], loss_sem,
                      (mid_idx, end_idx)[which], earlier)

    def loss_copy_same():
        return remote(loss_out, loss_in, loss_send.at[2], loss_sem, end_idx, stage)

    def normed_of(hidden_f32):
        inv_rms = lax.rsqrt(jnp.mean(hidden_f32 * hidden_f32, axis=-1, keepdims=True) + NORM_EPS)
        return inv_rms, (hidden_f32 * inv_rms * gain[...]).astype(BF16)

    def at(unit):
        return jnp.clip(unit, 0, units - 1)

    def fwd_iter(step, carry):
        @pl.when(is_mid & (step >= 2))
        def _():
            unit = at(step - 2)
            slot = lax.rem(unit, 2)
            sum_copy(unit, slot).wait_recv()
            sum_low_copy(unit, slot).wait_recv()
            total = s_out[slot].astype(F32) + s_in[2 * unit].astype(F32)
            c_fold = (sl_out[slot].astype(F32) + sl_in[2 * unit].astype(F32)).astype(BF16)
            c_s[unit] = c_fold
            c_copy(unit).start()
            mask_rows = mask[unit]
            delta = total + LORA_SCALE * dot_nn(unfold(c_fold, mask_rows), b_down[...])
            hidden = (h_in[unit].astype(F32) + delta).astype(BF16)

            @pl.when(stage < last)
            def _():
                @pl.when(unit >= 2)
                def _():
                    hidden_copy(at(unit - 2), slot, 0).wait_send()
                    hidden_copy(at(unit - 2), slot, 1).wait_send()

                h_out[slot] = hidden
                hidden_copy(unit, slot, 0).start()
                hidden_copy(unit, slot, 1).start()

            @pl.when(is_last)
            def _():
                residual = hidden.astype(F32) - g_in[unit].astype(F32)
                weighted = weight[unit][:, :1] * residual
                g_in[unit] = weighted.astype(BF16)
                top_copy(unit).start()
                row_sum = jnp.sum(weighted * residual, axis=-1, keepdims=True)
                loss_out[...] += jnp.broadcast_to(
                    jnp.sum(row_sum * mask_rows.astype(F32), axis=0, keepdims=True), loss_out.shape)

        @pl.when(is_mid & (step >= 1) & (step <= units))
        def _():
            unit = at(step - 1)
            slot = lax.rem(unit, 2)
            part_copy(unit, slot).wait_recv()
            part_low_copy(unit, slot).wait_recv()

            @pl.when(unit >= 2)
            def _():
                sum_copy(at(unit - 2), slot).wait_send()
                sum_low_copy(at(unit - 2), slot).wait_send()

            s_out[slot] = (part[slot, :, pl.ds(0, d_model)] + p_in[unit].astype(F32)).astype(BF16)
            sum_copy(unit, slot).start()
            sl_out[slot] = (part[slot, :, pl.ds(d_model, FOLD)] + pl_in[unit].astype(F32)).astype(BF16)
            sum_low_copy(unit, slot).start()

        @pl.when(step < units)
        def _():
            idx = at(step)
            slot = lax.rem(idx, 2)

            @pl.when(stage > 0)
            def _():
                hidden_copy(idx, slot, 0).wait_recv()

            _, normed = normed_of(h_in[idx].astype(F32))
            mask_rows = mask[idx]
            low = dot_nt(normed, a_up[...]).astype(BF16) * mask_rows
            low_s[idx] = low
            gate_pre = dot_nt(normed, w_gate[...])
            gate_s[idx] = gate_pre
            up_val = dot_nt(normed, w_up[...]) + LORA_SCALE * dot_nn(low, b_up[...])
            up_s[idx] = up_val
            prod = (gate_pre * jax.nn.sigmoid(gate_pre) * up_val).astype(BF16)
            down = dot_nn(prod, w_down[...])
            low_down = fold(dot_nt(prod, a_down[...]) * mask_rows.astype(F32))

            @pl.when(is_mid)
            def _():
                part[slot, :, pl.ds(0, d_model)] = down
                part[slot, :, pl.ds(d_model, FOLD)] = low_down

            @pl.when(is_end)
            def _():
                @pl.when(idx >= 2)
                def _():
                    part_copy(at(idx - 2), slot).wait_send()
                    part_low_copy(at(idx - 2), slot).wait_send()

                p_out[slot] = down.astype(BF16)
                part_copy(idx, slot).start()
                pl_out[slot] = low_down.astype(BF16)
                part_low_copy(idx, slot).start()

        return carry

    lax.fori_loop(0, units + 2, fwd_iter, 0)

    def bwd_iter(step, carry):
        @pl.when(is_mid & (step >= 2) & (step <= units + 1))
        def _():
            unit = at(step - 2)
            slot = lax.rem(unit, 2)
            sum_low_copy(unit, slot + 2).wait_recv()
            low_total = sl_out[slot + 2].astype(F32) + sl_in[2 * unit + 1].astype(F32)
            l_fold = (LORA_SCALE * low_total).astype(BF16)
            l_s[unit] = l_fold
            l_copy(unit).start()

            @pl.when(stage > 0)
            def _():
                sum_copy(unit, slot + 2).wait_recv()
                total = s_out[slot + 2].astype(F32) + s_in[2 * unit + 1].astype(F32)
                g_normed = total + dot_nn(unfold(l_fold, mask[unit]), a_up[...])
                hidden_f32 = h_in[unit].astype(F32)
                inv_rms = lax.rsqrt(jnp.mean(hidden_f32 * hidden_f32, axis=-1, keepdims=True) + NORM_EPS)
                g_scaled = g_normed * gain[...]
                unit_rows = hidden_f32 * inv_rms
                g_hidden = inv_rms * (g_scaled - unit_rows * jnp.mean(g_scaled * unit_rows, axis=-1, keepdims=True))

                @pl.when(unit >= 2)
                def _():
                    grad_copy(at(unit - 2), slot + 2, 0).wait_send()
                    grad_copy(at(unit - 2), slot + 2, 1).wait_send()

                h_out[slot + 2] = (g_in[unit].astype(F32) + g_hidden).astype(BF16)
                grad_copy(unit, slot + 2, 0).start()
                grad_copy(unit, slot + 2, 1).start()

        @pl.when(is_mid & (step >= 1) & (step <= units))
        def _():
            unit = at(step - 1)
            slot = lax.rem(unit, 2)
            part_low_copy(unit, slot + 2).wait_recv()

            @pl.when(unit >= 2)
            def _():
                sum_low_copy(at(unit - 2), slot + 2).wait_send()

            sl_out[slot + 2] = (part[slot, :, pl.ds(d_model, FOLD)] + pl_in[unit].astype(F32)).astype(BF16)
            sum_low_copy(unit, slot + 2).start()

            @pl.when(stage > 0)
            def _():
                part_copy(unit, slot + 2).wait_recv()

                @pl.when(unit >= 2)
                def _():
                    sum_copy(at(unit - 2), slot + 2).wait_send()

                s_out[slot + 2] = (part[slot, :, pl.ds(0, d_model)] + p_in[unit].astype(F32)).astype(BF16)
                sum_copy(unit, slot + 2).start()

        @pl.when(step < units)
        def _():
            idx = at(step)
            slot = lax.rem(idx, 2)

            @pl.when(jnp.logical_not(is_last & is_mid))
            def _():
                grad_copy(idx, slot + 2, 0).wait_recv()

            grad = g_in[idx]
            mask_rows = mask[idx]
            g_low = (LORA_SCALE * dot_nt(grad, b_down[...])).astype(BF16) * mask_rows
            gld_s[...] = g_low
            g_prod = dot_nt(grad, w_down[...]) + dot_nn(g_low, a_down[...])
            gate_pre = gate_s[idx]
            up_val = up_s[idx]
            sig = jax.nn.sigmoid(gate_pre)
            act = gate_pre * sig
            q_s[...] = (act * up_val).astype(BF16)
            g_up = (g_prod * act).astype(BF16)
            gup_s[...] = g_up
            g_gate = (g_prod * up_val * (sig * (1.0 + gate_pre * (1.0 - sig)))).astype(BF16)
            g_low_up = fold(dot_nt(g_up, b_up[...]) * mask_rows.astype(F32))

            @pl.when(is_mid)
            def _():
                part[slot, :, pl.ds(d_model, FOLD)] = g_low_up

            @pl.when(is_end)
            def _():
                @pl.when(idx >= 2)
                def _():
                    part_low_copy(at(idx - 2), slot + 2).wait_send()

                pl_out[slot + 2] = g_low_up.astype(BF16)
                part_low_copy(idx, slot + 2).start()

            @pl.when(stage > 0)
            def _():
                g_norm = dot_nn(g_gate, w_gate[...]) + dot_nn(g_up, w_up[...])

                @pl.when(is_mid)
                def _():
                    part[slot, :, pl.ds(0, d_model)] = g_norm

                @pl.when(is_end)
                def _():
                    @pl.when(idx >= 2)
                    def _():
                        part_copy(at(idx - 2), slot + 2).wait_send()

                    p_out[slot + 2] = g_norm.astype(BF16)
                    part_copy(idx, slot + 2).start()

        @pl.when(step < units)
        def _():
            idx = at(step)

            @pl.when(is_end)
            def _():
                c_copy(idx).wait_recv()

            mask_rows = mask[idx]
            g_low = gld_s[...]
            g_a_down[...] += dot_tn(g_low, q_s[...])[:used]
            g_b_up[...] += dot_tn(low_s[idx], gup_s[...])[:used]
            g_b_down[...] += dot_tn(unfold(c_s[idx], mask_rows), g_in[idx])[:used]

        @pl.when(step >= 3)
        def _():
            unit = at(step - 3)

            @pl.when(is_end)
            def _():
                l_copy(unit).wait_recv()

            _, normed = normed_of(h_in[unit].astype(F32))
            g_a_up[...] += dot_tn(unfold(l_s[unit], mask[unit]), normed)[:used]

        return carry

    lax.fori_loop(0, units + 3, bwd_iter, 0)
    g_b_up[...] = LORA_SCALE * g_b_up[...]
    g_b_down[...] = LORA_SCALE * g_b_down[...]

    @pl.when(is_mid & is_last)
    def _():
        loss_copy_same().start()

    @pl.when(jnp.logical_not(is_mid & is_last))
    def _():
        loss_copy(0).wait_recv()
        loss_out[...] = loss_in[...]

    @pl.when(is_mid & (stage > 0))
    def _():
        loss_copy(0).start()
        loss_copy(1).start()

    @pl.when(is_mid & is_last)
    def _():
        loss_copy_same().wait_send()

    @pl.when(is_mid & (stage > 0))
    def _():
        loss_copy(0).wait_send()
        loss_copy(1).wait_send()

    for unit in (units - 2, units - 1):
        slot = jnp.int32(unit % 2)

        @pl.when(is_end)
        def _():
            part_copy(unit, slot).wait_send()
            part_low_copy(unit, slot).wait_send()
            part_low_copy(unit, slot + 2).wait_send()

            @pl.when(stage > 0)
            def _():
                part_copy(unit, slot + 2).wait_send()

        @pl.when(is_mid)
        def _():
            sum_copy(unit, slot).wait_send()
            sum_low_copy(unit, slot).wait_send()
            sum_low_copy(unit, slot + 2).wait_send()

            @pl.when(stage < last)
            def _():
                hidden_copy(unit, slot, 0).wait_send()
                hidden_copy(unit, slot, 1).wait_send()

            @pl.when(stage > 0)
            def _():
                sum_copy(unit, slot + 2).wait_send()
                grad_copy(unit, slot + 2, 0).wait_send()
                grad_copy(unit, slot + 2, 1).wait_send()

    @pl.when(is_mid)
    def _():
        def drain(idx, carry):
            c_copy(idx).wait_send()
            l_copy(idx).wait_send()

            @pl.when(is_last)
            def _():
                top_copy(idx).wait_send()

            return carry

        lax.fori_loop(0, units, drain, 0)


def sweep(units, stages, weights, rows, mask, weight, collective_id):
    width, d_model = weights[0].shape
    used = weights[4].shape[0]
    msg = d_model + FOLD
    vmem = pl.BlockSpec(memory_space=pltpu.VMEM)
    out_shape = (
        jax.ShapeDtypeStruct((8, LANES), F32),
        jax.ShapeDtypeStruct((used, d_model), F32),
        jax.ShapeDtypeStruct((used, width), F32),
        jax.ShapeDtypeStruct((used, width), F32),
        jax.ShapeDtypeStruct((used, d_model), F32),
    )
    dma = pltpu.SemaphoreType.DMA
    return pl.pallas_call(
        functools.partial(sweep_kernel, units, stages),
        out_shape=out_shape,
        in_specs=[vmem] * 4 + [pl.BlockSpec(memory_space=pltpu.HBM)] * 5 + [vmem] * 2,
        out_specs=(vmem,) * 5,
        scratch_shapes=[
            pltpu.VMEM((units, UNIT, d_model), BF16),
            pltpu.VMEM((units, UNIT, d_model), BF16),
            pltpu.VMEM((units, UNIT, width), F32),
            pltpu.VMEM((units, UNIT, width), F32),
            pltpu.VMEM((units, UNIT, LANES), BF16),
            pltpu.VMEM((units, UNIT, FOLD), BF16),
            pltpu.VMEM((units, UNIT, FOLD), BF16),
            pltpu.VMEM((units, UNIT, d_model), BF16),
            pltpu.VMEM((units, UNIT, FOLD), BF16),
            pltpu.VMEM((2 * units, UNIT, d_model), BF16),
            pltpu.VMEM((2 * units, UNIT, FOLD), BF16),
            pltpu.VMEM((2, UNIT, msg), F32),
            pltpu.VMEM((4, UNIT, d_model), BF16),
            pltpu.VMEM((4, UNIT, FOLD), BF16),
            pltpu.VMEM((4, UNIT, d_model), BF16),
            pltpu.VMEM((4, UNIT, FOLD), BF16),
            pltpu.VMEM((4, UNIT, d_model), BF16),
            pltpu.VMEM((UNIT, width), BF16),
            pltpu.VMEM((UNIT, width), BF16),
            pltpu.VMEM((UNIT, LANES), BF16),
            pltpu.VMEM((8, LANES), F32),
            pltpu.VMEM((LANES, d_model), BF16),
            pltpu.VMEM((LANES, width), BF16),
            pltpu.VMEM((LANES, width), BF16),
            pltpu.VMEM((LANES, d_model), BF16),
            dma,
            dma((4,)),
            dma((units,)),
            dma((units,)),
            dma((2 * units,)),
            dma((2 * units,)),
            dma((units,)),
            dma((units,)),
            dma((units,)),
            dma((units,)),
            dma,
            dma((4,)),
            dma((4,)),
            dma((4,)),
            dma((4,)),
            dma((4, 2)),
            dma((units,)),
            dma((units,)),
            dma((units,)),
            dma((3,)),
        ],
        compiler_params=pltpu.CompilerParams(collective_id=collective_id, has_side_effects=True,
                                             vmem_limit_bytes=66_000_000),
    )(*weights, rows, mask, weight)


def solution(mesh):
    num_stages = mesh.shape["pp"]

    def stage_body(w_gate, w_up, w_down, norm_gain, a_up, b_up, a_down, b_down, inputs, targets, lengths):
        stage_idx = lax.axis_index("pp")
        num_jobs, num_micro, row_count, seq_len, d_model = inputs.shape
        rank = a_up.shape[-1]
        job_rows = num_micro * row_count
        num_rows = num_jobs * job_rows
        num_tokens = num_rows * seq_len
        width = w_gate.shape[-1]
        used = num_jobs * rank

        order = np.arange(num_rows).reshape(lengths.shape)
        row_lens = jnp.sum(jnp.where(np.arange(num_rows)[:, None, None, None] == order[None], lengths[None], 0), axis=(1, 2, 3))
        row_ends = jnp.cumsum(row_lens)
        row_starts = row_ends - row_lens
        job_norms = jnp.sum(lengths, axis=(1, 2)).astype(F32) * d_model
        row_jobs = jnp.arange(num_rows) // job_rows
        row_shift = jnp.arange(num_rows) * seq_len - row_starts
        row_weight = jnp.repeat(1.0 / job_norms, job_rows)

        a_up_all = jnp.swapaxes(a_up[0], 1, 2).reshape(used, d_model)
        b_up_all = b_up[0].reshape(used, width)
        a_down_all = jnp.swapaxes(a_down[0], 1, 2).reshape(used, width)
        b_down_all = b_down[0].reshape(used, d_model)
        gain = jnp.broadcast_to(norm_gain.astype(F32), (UNIT, d_model))
        weights = (jnp.swapaxes(w_gate[0], 0, 1), jnp.swapaxes(w_up[0], 0, 1), w_down[0], gain, a_up_all, b_up_all, a_down_all, b_down_all)
        rows_all = jnp.where(stage_idx == num_stages - 1, targets, inputs).reshape(num_tokens, d_model)

        def run(plan):
            def one_pass(units, first):
                slots = first + jnp.arange(units * UNIT)
                in_row = (slots[:, None] >= row_starts[None, :]) & (slots[:, None] < row_ends[None, :])
                valid = slots < row_ends[-1]
                source = slots + jnp.sum(jnp.where(in_row, row_shift[None, :], 0), axis=1)
                job = jnp.sum(jnp.where(in_row, row_jobs[None, :], 0), axis=1)
                weight = jnp.sum(jnp.where(in_row, row_weight[None, :], 0.0), axis=1)
                pick = ((source[:, None] == jnp.arange(num_tokens)[None, :]) & valid[:, None]).astype(BF16)
                rows = jnp.dot(pick, rows_all, preferred_element_type=F32).astype(BF16)
                mask = ((jnp.arange(LANES)[None, :] // rank == job[:, None]) & valid[:, None]).astype(BF16)
                return sweep(units, num_stages, weights,
                             rows.reshape(units, UNIT, d_model), mask.reshape(units, UNIT, LANES),
                             jnp.broadcast_to(weight[:, None], (units * UNIT, FOLD)).reshape(units, UNIT, FOLD), 0)

            if len(plan) == 1:
                return tuple(one_pass(plan[0], 0))
            zeros = tuple(jnp.zeros(shape, F32) for shape in ((8, LANES), (used, d_model), (used, width), (used, width), (used, d_model)))
            return lax.fori_loop(0, len(plan), lambda turn, outs: tuple(
                old + add for old, add in zip(outs, one_pass(plan[0], turn * plan[0] * UNIT))), zeros)

        caps = [sum(plan) * UNIT for plan in PLANS]
        choice = sum((row_ends[-1] > cap).astype(jnp.int32) for cap in caps[:-1])
        loss, g_a_up, g_b_up, g_a_down, g_b_down = lax.switch(choice, [functools.partial(run, plan) for plan in PLANS])
        losses = 0.5 * loss[0, :used:rank]
        g_a_up = jnp.swapaxes(g_a_up.reshape(1, num_jobs, rank, d_model), 2, 3)
        g_b_up = g_b_up.reshape(1, num_jobs, rank, width)
        g_a_down = jnp.swapaxes(g_a_down.reshape(1, num_jobs, rank, width), 2, 3)
        g_b_down = g_b_down.reshape(1, num_jobs, rank, d_model)
        return losses, g_a_up, g_b_up, g_a_down, g_b_down

    weight_specs = (P("pp", None, "tp"), P("pp", None, "tp"), P("pp", "tp", None), P("pp", None))
    adapter_specs = (P("pp", "rep", None, None), P("pp", "rep", None, "tp"), P("pp", "rep", "tp", None), P("pp", "rep", None, None))
    data_specs = (P("rep"), P("rep"), P("rep"))
    return jax.shard_map(stage_body, mesh=mesh, in_specs=weight_specs + adapter_specs + data_specs,
                         out_specs=(P("rep"),) + adapter_specs, check_vma=False)
```

profile of v0, /device:TPU:2, one launch (start us, length us, event | category | flops | bytes accessed | tf_op | source)
XLA Modules:
  0.0 335.0 jit_solution(3421831036213404362)
XLA Ops:
  0.6 0.8 copy.21
  1.4 0.8 select_reduce_fusion.9
  2.2 0.1 copy.22
  2.3 0.1 reduce-window.4
  2.4 0.1 reduce.3
  2.5 0.7 convert_element_type.60
  3.2 0.7 reduce_sum.127
  4.0 0.5 slice.36
  5.8 319.5 %conditional.1 = (f32[192,896]{1,0:T(8,128)}, f32[192,1216]{1,0:T(8,128)}, f32[192,1216]{1,0:T(8,128)}, f32[192,896]{1,0:T(8,128)}, f32[8,256]{1,0:T(8,128)}) conditional(s32[]{:T(128)} %bitcast.27, (bf16[1,1216,896]{2,1,0:T(8,128)(2,1)}, f32[1,896]{1,0:T(1,128)S(1)}, bf16[6,32,896]{2,1,0:T(8,128)(2,1)}, ...), branch_computations={%region_3.7_spmd, %region_7.11_spmd, %region_11.17_spmd} | conditional | flops 6354155008 | bytes 39319136 | solution.py:610
  6.0 0.1 and_select_fusion.3
  6.1 0.2 select_reduce_fusion.7
  6.3 0.6 slice.29
  6.9 0.7 iota_compare_fusion.8
  7.6 2.6 broadcast_select_fusion.1
  10.2 0.0 copy-start.1
  10.2 0.0 copy-start.4
  10.2 9.3 %fusion.28 = bf16[1536,896]{1,0:T(8,128)(2,1)} fusion(bf16[2304,896]{1,0:T(8,128)(2,1)S(1)} %bitcast.97, s32[1536]{0:T(1024)S(1)} %iota_add_fusion.2, pred[1536]{0:T(1024)(128)(4,1)S(1)} %iota_compare_fusion.8), kind=kOutput, calls=%fused_computation.56 | convolution fusion | flops 6350241792 | bytes 6888960 | tf_op jit(solution)/shard_map/cond/branch_1_fun/dot_general | solution.py:596
  19.5 0.7 add_compare_fusion.2
  20.2 1.3 and_convert_fusion.2.mask
  21.5 0.1 broadcast_in_dim.282
  21.6 0.1 broadcast_in_dim.283
  21.7 0.1 select_reduce_fusion.6
  21.8 1.1 broadcast_in_dim.287.weight
  23.0 0.8 broadcast_in_dim.278.gain
  23.8 0.0 copy-done.1
  23.8 0.0 copy-done.4
  23.8 301.0 %branch_1_fun.2 = (f32[8,256]{1,0:T(8,128)}, f32[192,896]{1,0:T(8,128)}, f32[192,1216]{1,0:T(8,128)}, f32[192,1216]{1,0:T(8,128)}, f32[192,896]{1,0:T(8,128)}) custom-call(bf16[1216,896]{1,0:T(8,128)(2,1)} %get-tuple-element.827.w_gate, bf16[1216,896]{1,0:T(8,128)(2,1)} %get-tuple-element.828.w_up, bf16[1216,896]{1,0:T(8,128)(2,1)} %bitcast.68, ...), custom_call_target="tpu_custom_call" | custom-call | tf_op jit(solution)/shard_map/cond/branch_1_fun/pallas_call | solution.py:500
  325.3 0.8 slice.34
  326.1 0.5 multiply_bitcast_fusion
  326.6 2.0 copy.60
  328.6 2.2 copy.61
  330.8 2.2 copy.62
  333.0 2.0 copy.63
  (10 shorter events, 0.1 us)
Async XLA Ops:
  10.2 13.6 %copy-start.1 = (bf16[1,6,32,1216]{3,2,1,0:T(8,128)(2,1)S(1)}, bf16[1,6,32,1216]{3,2,1,0:T(8,128)(2,1)}, u32[]{:S(2)}) copy-start(bf16[1,6,32,1216]{3,2,1,0:T(8,128)(2,1)} %get-tuple-element.832) | copy-start | bytes 1400836 | tf_op jit(solution)/shard_map/cond
  10.2 13.6 %copy-start.4 = (bf16[6,32,1216]{2,1,0:T(8,128)(2,1)S(1)}, bf16[6,32,1216]{2,1,0:T(8,128)(2,1)}, u32[]{:S(2)}) copy-start(bf16[6,32,1216]{2,1,0:T(8,128)(2,1)} %get-tuple-element.833) | copy-start | bytes 1400836 | tf_op jit(solution)/shard_map/cond
where the time goes:
time: 335 us
  Pallas kernels  301 us (90%)
  local copies, waits for them, and re-layouts  13.3 us (4%)
  matrix products  9.31 us (3%)
  other arithmetic  8.63 us (3%)
    pallas_call x1, Pallas kernels, sweep(): pl.pallas_call(functools.partial(sweep_kernel, units, stages), out_shape=...  301 us
    dot_general x1, matrix products, one_pass(): rows = jnp.dot(pick, rows_all, preferred_element_type=F32).astype(BF16)  9.31 us
    unnamed x5, local copies, waits for them, and re-layouts  9.18 us

commit v1 on v0

--- a/solution.py
+++ b/solution.py
@@ -42,7 +42,7 @@
 def sweep_kernel(units, stages,
                  w_gate, w_up, w_down, gain, a_up_hbm, b_up_hbm, a_down_hbm, b_down_hbm, rows_hbm, mask, weight,
                  loss_out, g_a_up, g_b_up, g_a_down, g_b_down,
-                 h_in, g_in, gate_s, up_s, low_s, c_s, l_s, p_in, pl_in, s_in, sl_in, part, p_out, pl_out, s_out, sl_out, h_out, q_s, gup_s, gld_s, loss_in,
+                 h_in, g_in, gate_s, up_s, low_s, c_s, l_s, p_in, pl_in, s_in, sl_in, part, p_out, pl_out, s_out, sl_out, h_out, q_s, gup_s, ggate_s, gld_s, loss_in,
                  a_up, b_up, a_down, b_down, load_sem, adapter_sem, p_sem, pl_sem, s_sem, sl_sem, h_sem, g_sem, c_sem, l_sem, loss_sem,
                  p_send, pl_send, s_send, sl_send, h_send, c_send, l_send, g_send, loss_send):
     d_model = h_in.shape[2]
@@ -182,6 +182,25 @@
         return jnp.clip(unit, 0, units - 1)
 
     def fwd_iter(step, carry):
+        @pl.when(step < units)
+        def _():
+            idx = at(step)
+            slot = lax.rem(idx, 2)
+
+            @pl.when(stage > 0)
+            def _():
+                hidden_copy(idx, slot, 0).wait_recv()
+
+            _, normed = normed_of(h_in[idx].astype(F32))
+            mask_rows = mask[idx]
+            low = dot_nt(normed, a_up[...]).astype(BF16) * mask_rows
+            low_s[idx] = low
+            gate_pre = dot_nt(normed, w_gate[...])
+            gate_s[idx] = gate_pre
+            up_val = dot_nt(normed, w_up[...]) + LORA_SCALE * dot_nn(low, b_up[...])
+            up_s[idx] = up_val
+            q_s[...] = (gate_pre * jax.nn.sigmoid(gate_pre) * up_val).astype(BF16)
+
         @pl.when(is_mid & (step >= 2))
         def _():
             unit = at(step - 2)
@@ -238,22 +257,9 @@
         def _():
             idx = at(step)
             slot = lax.rem(idx, 2)
-
-            @pl.when(stage > 0)
-            def _():
-                hidden_copy(idx, slot, 0).wait_recv()
-
-            _, normed = normed_of(h_in[idx].astype(F32))
-            mask_rows = mask[idx]
-            low = dot_nt(normed, a_up[...]).astype(BF16) * mask_rows
-            low_s[idx] = low
-            gate_pre = dot_nt(normed, w_gate[...])
-            gate_s[idx] = gate_pre
-            up_val = dot_nt(normed, w_up[...]) + LORA_SCALE * dot_nn(low, b_up[...])
-            up_s[idx] = up_val
-            prod = (gate_pre * jax.nn.sigmoid(gate_pre) * up_val).astype(BF16)
+            prod = q_s[...]
             down = dot_nn(prod, w_down[...])
-            low_down = fold(dot_nt(prod, a_down[...]) * mask_rows.astype(F32))
+            low_down = fold(dot_nt(prod, a_down[...]) * mask[idx].astype(F32))
 
             @pl.when(is_mid)
             def _():
@@ -277,60 +283,6 @@
     lax.fori_loop(0, units + 2, fwd_iter, 0)
 
     def bwd_iter(step, carry):
-        @pl.when(is_mid & (step >= 2) & (step <= units + 1))
-        def _():
-            unit = at(step - 2)
-            slot = lax.rem(unit, 2)
-            sum_low_copy(unit, slot + 2).wait_recv()
-            low_total = sl_out[slot + 2].astype(F32) + sl_in[2 * unit + 1].astype(F32)
-            l_fold = (LORA_SCALE * low_total).astype(BF16)
-            l_s[unit] = l_fold
-            l_copy(unit).start()
-
-            @pl.when(stage > 0)
-            def _():
-                sum_copy(unit, slot + 2).wait_recv()
-                total = s_out[slot + 2].astype(F32) + s_in[2 * unit + 1].astype(F32)
-                g_normed = total + dot_nn(unfold(l_fold, mask[unit]), a_up[...])
-                hidden_f32 = h_in[unit].astype(F32)
-                inv_rms = lax.rsqrt(jnp.mean(hidden_f32 * hidden_f32, axis=-1, keepdims=True) + NORM_EPS)
-                g_scaled = g_normed * gain[...]
-                unit_rows = hidden_f32 * inv_rms
-                g_hidden = inv_rms * (g_scaled - unit_rows * jnp.mean(g_scaled * unit_rows, axis=-1, keepdims=True))
-
-                @pl.when(unit >= 2)
-                def _():
-                    grad_copy(at(unit - 2), slot + 2, 0).wait_send()
-                    grad_copy(at(unit - 2), slot + 2, 1).wait_send()
-
-                h_out[slot + 2] = (g_in[unit].astype(F32) + g_hidden).astype(BF16)
-                grad_copy(unit, slot + 2, 0).start()
-                grad_copy(unit, slot + 2, 1).start()
-
-        @pl.when(is_mid & (step >= 1) & (step <= units))
-        def _():
-            unit = at(step - 1)
-            slot = lax.rem(unit, 2)
-            part_low_copy(unit, slot + 2).wait_recv()
-
-            @pl.when(unit >= 2)
-            def _():
-                sum_low_copy(at(unit - 2), slot + 2).wait_send()
-
-            sl_out[slot + 2] = (part[slot, :, pl.ds(d_model, FOLD)] + pl_in[unit].astype(F32)).astype(BF16)
-            sum_low_copy(unit, slot + 2).start()
-
-            @pl.when(stage > 0)
-            def _():
-                part_copy(unit, slot + 2).wait_recv()
-
-                @pl.when(unit >= 2)
-                def _():
-                    sum_copy(at(unit - 2), slot + 2).wait_send()
-
-                s_out[slot + 2] = (part[slot, :, pl.ds(0, d_model)] + p_in[unit].astype(F32)).astype(BF16)
-                sum_copy(unit, slot + 2).start()
-
         @pl.when(step < units)
         def _():
             idx = at(step)
@@ -352,7 +304,7 @@
             q_s[...] = (act * up_val).astype(BF16)
             g_up = (g_prod * act).astype(BF16)
             gup_s[...] = g_up
-            g_gate = (g_prod * up_val * (sig * (1.0 + gate_pre * (1.0 - sig)))).astype(BF16)
+            ggate_s[...] = (g_prod * up_val * (sig * (1.0 + gate_pre * (1.0 - sig)))).astype(BF16)
             g_low_up = fold(dot_nt(g_up, b_up[...]) * mask_rows.astype(F32))
 
             @pl.when(is_mid)
@@ -368,8 +320,69 @@
                 pl_out[slot + 2] = g_low_up.astype(BF16)
                 part_low_copy(idx, slot + 2).start()
 
+        @pl.when(is_mid & (step >= 2) & (step <= units + 1))
+        def _():
+            unit = at(step - 2)
+            slot = lax.rem(unit, 2)
+            sum_low_copy(unit, slot + 2).wait_recv()
+            low_total = sl_out[slot + 2].astype(F32) + sl_in[2 * unit + 1].astype(F32)
+            l_fold = (LORA_SCALE * low_total).astype(BF16)
+            l_s[unit] = l_fold
+            l_copy(unit).start()
+
             @pl.when(stage > 0)
             def _():
+                sum_copy(unit, slot + 2).wait_recv()
+                total = s_out[slot + 2].astype(F32) + s_in[2 * unit + 1].astype(F32)
+                g_normed = total + dot_nn(unfold(l_fold, mask[unit]), a_up[...])
+                hidden_f32 = h_in[unit].astype(F32)
+                inv_rms = lax.rsqrt(jnp.mean(hidden_f32 * hidden_f32, axis=-1, keepdims=True) + NORM_EPS)
+                g_scaled = g_normed * gain[...]
+                unit_rows = hidden_f32 * inv_rms
+                g_hidden = inv_rms * (g_scaled - unit_rows * jnp.mean(g_scaled * unit_rows, axis=-1, keepdims=True))
+
+                @pl.when(unit >= 2)
+                def _():
+                    grad_copy(at(unit - 2), slot + 2, 0).wait_send()
+                    grad_copy(at(unit - 2), slot + 2, 1).wait_send()
+
+                h_out[slot + 2] = (g_in[unit].astype(F32) + g_hidden).astype(BF16)
+                grad_copy(unit, slot + 2, 0).start()
+                grad_copy(unit, slot + 2, 1).start()
+
+        @pl.when(is_mid & (step >= 1) & (step <= units))
+        def _():
+            unit = at(step - 1)
+            slot = lax.rem(unit, 2)
+            part_low_copy(unit, slot + 2).wait_recv()
+
+            @pl.when(unit >= 2)
+            def _():
+                sum_low_copy(at(unit - 2), slot + 2).wait_send()
+
+            sl_out[slot + 2] = (part[slot, :, pl.ds(d_model, FOLD)] + pl_in[unit].astype(F32)).astype(BF16)
+            sum_low_copy(unit, slot + 2).start()
+
+            @pl.when(stage > 0)
+            def _():
+                part_copy(unit, slot + 2).wait_recv()
+
+                @pl.when(unit >= 2)
+                def _():
+                    sum_copy(at(unit - 2), slot + 2).wait_send()
+
+                s_out[slot + 2] = (part[slot, :, pl.ds(0, d_model)] + p_in[unit].astype(F32)).astype(BF16)
+                sum_copy(unit, slot + 2).start()
+
+        @pl.when(step < units)
+        def _():
+            idx = at(step)
+            slot = lax.rem(idx, 2)
+
+            @pl.when(stage > 0)
+            def _():
+                g_gate = ggate_s[...]
+                g_up = gup_s[...]
                 g_norm = dot_nn(g_gate, w_gate[...]) + dot_nn(g_up, w_up[...])
 
                 @pl.when(is_mid)
@@ -522,6 +535,7 @@
             pltpu.VMEM((4, UNIT, d_model), BF16),
             pltpu.VMEM((UNIT, width), BF16),
             pltpu.VMEM((UNIT, width), BF16),
+            pltpu.VMEM((UNIT, width), BF16),
             pltpu.VMEM((UNIT, LANES), BF16),
             pltpu.VMEM((8, LANES), F32),
             pltpu.VMEM((LANES, d_model), BF16),

time: 335 us -> 308 us (0.919)
  the two profiles are of different devices: /device:TPU:2 before, /device:TPU:0 now
where the time goes in v1:
time: 308 us; the launch traced here: 307 us
  Pallas kernels  275 us (89%)
  local copies, waits for them, and re-layouts  13.2 us (4%)
  other arithmetic  8.51 us (3%)
  matrix products  7.95 us (3%)
    pallas_call x1, Pallas kernels, sweep(): pl.pallas_call(functools.partial(sweep_kernel, units, stages), out_shape=...  275 us
    unnamed x5, local copies, waits for them, and re-layouts  9.18 us
    dot_general x1, matrix products, one_pass(): rows = jnp.dot(pick, rows_all, preferred_element_type=F32).astype(BF16)  7.95 us

profile of v1, /device:TPU:0, one launch (start us, length us, event | category | flops | bytes accessed | tf_op | source)
XLA Modules:
  0.0 307.2 jit_solution(5889469762771209031)
XLA Ops:
  0.6 0.8 copy.21
  1.4 0.8 select_reduce_fusion.9
  2.2 0.1 copy.22
  2.3 0.1 reduce-window.4
  2.4 0.1 reduce.3
  2.5 0.7 convert_element_type.60
  3.2 0.7 reduce_sum.127
  4.0 0.5 slice.36
  5.8 291.8 %conditional.1 = (f32[192,896]{1,0:T(8,128)}, f32[192,1216]{1,0:T(8,128)}, f32[192,1216]{1,0:T(8,128)}, f32[192,896]{1,0:T(8,128)}, f32[8,256]{1,0:T(8,128)}) conditional(s32[]{:T(128)} %bitcast.27, (bf16[1,1216,896]{2,1,0:T(8,128)(2,1)}, f32[1,896]{1,0:T(1,128)S(1)}, bf16[6,32,896]{2,1,0:T(8,128)(2,1)}, ...), branch_computations={%region_3.7_spmd, %region_7.11_spmd, %region_11.17_spmd} | conditional | flops 6354155008 | bytes 39319136 | solution.py:624
  5.8 0.1 and_select_fusion.1
  5.9 0.1 select_reduce_fusion.4
  6.1 0.6 slice.28
  6.7 0.7 iota_compare_fusion.4
  7.3 2.6 broadcast_select_fusion
  9.9 0.0 copy-start
  10.0 0.0 copy-start.3
  10.0 8.0 %fusion.19 = bf16[1280,896]{1,0:T(8,128)(2,1)} fusion(bf16[2304,896]{1,0:T(8,128)(2,1)S(1)} %bitcast.96, s32[1280]{0:T(1024)S(1)} %iota_add_fusion.1, pred[1280]{0:T(1024)(128)(4,1)S(1)} %iota_compare_fusion.4), kind=kOutput, calls=%fused_computation.32 | convolution fusion | flops 5291868160 | bytes 6428928 | tf_op jit(solution)/shard_map/cond/branch_0_fun/dot_general | solution.py:610
  17.9 0.7 add_compare_fusion.1
  18.6 1.3 and_convert_fusion.1.mask
  19.8 0.1 broadcast_in_dim.271
  19.9 0.1 broadcast_in_dim.272
  20.0 0.1 select_reduce_fusion.3
  20.1 1.1 broadcast_in_dim.276.weight
  21.2 0.8 broadcast_in_dim.267.gain
  22.0 0.0 copy-done
  22.0 0.0 copy-done.3
  22.0 275.3 %branch_0_fun.2 = (f32[8,256]{1,0:T(8,128)}, f32[192,896]{1,0:T(8,128)}, f32[192,1216]{1,0:T(8,128)}, f32[192,1216]{1,0:T(8,128)}, f32[192,896]{1,0:T(8,128)}) custom-call(bf16[1216,896]{1,0:T(8,128)(2,1)} %get-tuple-element.804.w_gate, bf16[1216,896]{1,0:T(8,128)(2,1)} %get-tuple-element.805.w_up, bf16[1216,896]{1,0:T(8,128)(2,1)} %bitcast.67, ...), custom_call_target="tpu_custom_call" | custom-call | tf_op jit(solution)/shard_map/cond/branch_0_fun/pallas_call | solution.py:513
  297.5 0.8 slice.34
  298.3 0.5 multiply_bitcast_fusion
  298.8 2.0 copy.60
  300.8 2.2 copy.61
  303.0 2.2 copy.62
  305.3 2.0 copy.63
  (10 shorter events, 0.1 us)
Async XLA Ops:
  9.9 12.1 %copy-start = (bf16[1,6,32,1216]{3,2,1,0:T(8,128)(2,1)S(1)}, bf16[1,6,32,1216]{3,2,1,0:T(8,128)(2,1)}, u32[]{:S(2)}) copy-start(bf16[1,6,32,1216]{3,2,1,0:T(8,128)(2,1)} %get-tuple-element.809) | copy-start | bytes 1400836 | tf_op jit(solution)/shard_map/cond
  10.0 12.1 %copy-start.3 = (bf16[6,32,1216]{2,1,0:T(8,128)(2,1)S(1)}, bf16[6,32,1216]{2,1,0:T(8,128)(2,1)}, u32[]{:S(2)}) copy-start(bf16[6,32,1216]{2,1,0:T(8,128)(2,1)} %get-tuple-element.810) | copy-start | bytes 1400836 | tf_op jit(solution)/shard_map/cond
